TPU v7x, 128 devices: a whole 4x4x4 slice. The times are simulated.
128 devices in a mesh: ens: 1, part: 16 (over z, y), feat: 8 (over x, core).
Axes of the slice: x: 4, y: 4, z: 4, core: 2. Of those that a mesh axis runs over, the one named last changes fastest.
Arguments:
- particles: float32 [2048, 32768], P(('ens', 'part'), 'feat')
- prec_diag: float32 [32768], P(('ens', 'feat'))
- target_mean: float32 [32768], P(('ens', 'feat'))
- low_factor: bfloat16 [32768, 64], P(('ens', 'feat'))
Outputs:
- output: float32 [2048, 32768], P(('ens', 'part'), 'feat')
All inputs are finite; a program needn't handle non-finite values.
Results may differ from a plain program's by a relative error of at most 0.00350775.
Values are sent between devices in bfloat16 or wider.
A program may use at most 1 GiB of HBM per device.

v0:
```python
import functools
import math
import jax
import jax.numpy as jnp
from jax import lax
from jax.experimental import pallas as pl
from jax.experimental.pallas import tpu as pltpu
from jax.sharding import PartitionSpec as P

NUM_STEPS = 3
B = 128
PIECE = 48
F32 = jnp.float32
BF16 = jnp.bfloat16
NT = (((1,), (1,)), ((), ()))
TN = (((0,), (0,)), ((), ()))
NUM_SEMS = 416
PANEL = 512


def rem(a, n):
    return lax.rem(a, jnp.int32(n))


def div(a, n):
    return lax.div(a, jnp.int32(n))


def unrolled(count, by, body):
    def several(r, cc):
        for t in range(by):
            body(r * by + t)
        return cc
    lax.fori_loop(0, count // by, several, 0)


def mine(ref, h, v, src_at):
    hb = B // 2
    return ref.at[src_at, v, pl.ds(0, hb)] if h == 0 else ref.at[v, src_at, pl.ds(hb, hb)]


def steps_kernel(cfg, theta_ref, lam_all, mu_all, fact_all, out_ref, th, l1, m1, rel1, rel2, rel3, lam_ref, mu_ref, fact_ref,
                 t_own, t_par, a_buf, zt, zt_par, zt_b, s_all, d_all, g, ring1, relb, dirb, dir3, acc2, acc3, unit, ag,
                 ag_par, kfull, send_sems, recv_sems):
    nb, kern_width, step_size = cfg["nb"], cfg["kern_width"], cfg["step_size"]
    n_total = nb * B
    n_chip = 64
    part, feat = lax.axis_index("part"), lax.axis_index("feat")
    core = rem(feat, 2)
    me = (div(feat, 2), rem(part, 4), div(part, 4))
    near = [[me[d]] + [rem(me[d] + by, 4) for by in (1, 2, 3)] for d in range(3)]

    def dev(coord, c):
        return {"part": coord[2] * 4 + coord[1], "feat": coord[0] * 2 + c}

    def device_at(dim, by):
        c = list(me)
        c[dim] = near[dim][by]
        return dev(c, core)

    around = [[device_at(d, by) for by in range(4)] for d in range(3)]

    def shifted(dim, by):
        return around[dim][by]

    partner = dev(me, 1 - core)
    perms = [(k, (k + 1) % 3, (k + 2) % 3) for k in range(3)]

    ids = {}

    def slot_of(key):
        idx = ids.setdefault(key, len(ids))
        assert idx < NUM_SEMS - 8
        return idx

    def copy(key, src, dst, to):
        idx = slot_of(key)
        return pltpu.make_async_remote_copy(
            src_ref=src, dst_ref=dst, send_sem=send_sems.at[idx], recv_sem=recv_sems.at[idx],
            device_id=to, device_id_type=pl.DeviceIdType.MESH)

    def local(key, src, dst):
        return pltpu.make_async_copy(src, dst, send_sems.at[slot_of(key)])

    barrier = pltpu.get_barrier_semaphore()
    peers = [partner] + [shifted(d, by) for d in range(3) for by in (1, 2, 3)]
    for peer in peers:
        pl.semaphore_signal(barrier, inc=1, device_id=peer, device_id_type=pl.DeviceIdType.MESH)
    pl.semaphore_wait(barrier, len(peers))

    row = lax.broadcasted_iota(jnp.int32, (B, B), 0)
    col = lax.broadcasted_iota(jnp.int32, (B, B), 1)
    low, eye = row >= col, row == col

    def blk(i):
        return pl.ds(pl.multiple_of(i * B, B), B)

    def unit_of(c, q):
        u = c * n_chip + q
        i = rem(u, nb)
        return u, i, rem(i + div(u, nb) + 1, nb), u >= 2 * n_chip - nb // 2

    def chip_index(k, x, y, z):
        p = perms[k]
        c = (x, y, z)
        return (c[p[0]] * 4 + c[p[1]]) * 4 + c[p[2]]

    def split(n, wide):
        if n > 1:
            return (0, n // 2, 0, PIECE), (n // 2, n // 2, 0, PIECE)
        r = 32 if wide else 24
        return (0, 1, 0, r), (0, 1, r, PIECE - r)

    def part_of(ref, lead, base, half):
        return ref.at[lead, pl.ds(base + half[0], half[1]), pl.ds(half[2], half[3])]

    zh = zt.shape[0] // 2
    kc = nb // 4
    n_panels = n_total // PANEL

    def panel(r):
        return pl.ds(pl.multiple_of(r * PANEL, PANEL), PANEL)

    def swap_t(r, slot):
        return pltpu.make_async_remote_copy(
            src_ref=t_own.at[slot, panel(r)], dst_ref=t_par.at[panel(r)], send_sem=send_sems.at[NUM_SEMS - 1 - r],
            recv_sem=recv_sems.at[NUM_SEMS - 1 - r], device_id=partner, device_id_type=pl.DeviceIdType.MESH)

    def swap_z(r):
        return pltpu.make_async_remote_copy(
            src_ref=zt.at[pl.ds(pl.multiple_of((1 - core) * zh, 8), zh), panel(r)], dst_ref=zt_par.at[pl.ds(0, zh), panel(r)],
            send_sem=send_sems.at[NUM_SEMS - 1 - n_panels - r], recv_sem=recv_sems.at[NUM_SEMS - 1 - n_panels - r],
            device_id=partner, device_id_type=pl.DeviceIdType.MESH)

    def prepare(r, theta, slot):
        t_own[slot, panel(r)] = theta.astype(BF16)
        swap_t(r, slot).start()
        xb = (theta - mu_ref[...]).astype(BF16)
        zt[:, panel(r)] = lax.dot_general(fact_ref[...], xb, NT, preferred_element_type=F32)
        swap_z(r).start()

    def get_rows(r):
        return jnp.concatenate([th[r, v] for v in range(4)], 0)

    def first_prep(r, cc):
        prepare(r, get_rows(r), 0)
        return cc
    fcol, hb = fact_ref.shape[1], B // 2
    my = pl.ds(pl.multiple_of((me[1] * 4 + me[2]) * fcol, fcol), fcol)

    def cols(y, z, n=1):
        return pl.ds(pl.multiple_of((y * 4 + z) * fcol, fcol), n * fcol)

    def side(d, by):
        return near[d][by]

    def relayed(key, d, sends, begin=True):
        def copies(tag):
            return [copy((key, tag, t), src, dst, shifted(d, 1 if tag[1] == "+" else 3))
                    for t, (src, dst) in enumerate(sends(tag))]
        started = []

        def go(tags):
            for tag in tags:
                for m in copies(tag):
                    m.start()
                    started.append(m)

        def relay():
            for got, out in (("r+", "f+"), ("r-", "f-")):
                for m in copies(got):
                    m.wait_recv()
                go((out,))

        def finish():
            for tag in ("d+", "d-", "f+", "f-"):
                for m in copies(tag):
                    m.wait_recv()
        if begin:
            go(("r+", "r-", "d+", "d-"))
        else:
            for tag in ("r+", "r-", "d+", "d-"):
                started += copies(tag)
        return (relay, finish, started) if begin else (relay, finish, started, copies)

    def halves(tag):
        if tag[0] == "d":
            return (0, 1, 2, 3)
        return (0, 1) if tag[1] == "+" else (2, 3)

    def in_first(h):
        d = 1 + h

        def sends(tag):
            r0, nr = {"r+": (0, hb // 2), "r-": (hb // 2, hb // 2)}.get(tag, (0, hb))
            way = tag[1] == "+"
            if tag[0] == "f":
                b = 0 if way else 1
                return [(rel1.at[h, b], l1.at[h, side(d, 3 if way else 1), pl.ds(b * (hb // 2), hb // 2)])]
            to = side(d, {"r": 2, "d": 1 if way else 3}[tag[0]])
            rows = pl.ds(h * hb + r0, nr)

            def dst(y, n):
                at = pl.ds(y * fcol, n * fcol)
                if tag[0] == "d":
                    return l1.at[h, me[d], pl.ds(0, nr), at]
                return rel1.at[h, 0 if way else 1, pl.ds(0, nr), at]
            if h == 0:
                return [(theta_ref.at[rows, cols(to, 0, 4)], dst(0, 4))]
            return [(theta_ref.at[rows, cols(y, to)], dst(y, 1)) for y in range(4)]
        return relayed(("in1", h), d, sends)

    def in_second(h):
        d = 2 - h

        def sends(tag):
            way = tag[1] == "+"
            b = 0 if way else 1
            if tag[0] == "f":
                return [(rel2.at[h, b, v % 2], mine(th, h, v, side(d, 3 if way else 1))) for v in halves(tag)]
            to = side(d, {"r": 2, "d": 1 if way else 3}[tag[0]])
            at = pl.ds(pl.multiple_of(to * fcol, fcol), fcol)
            return [(l1.at[h, v, pl.ds(0, hb), at], mine(th, h, v, me[d]) if tag[0] == "d" else rel2.at[h, b, v % 2])
                    for v in halves(tag)]
        return relayed(("in2", h), d, sends)

    own_in = [local(("own", 0), theta_ref.at[pl.ds(0, hb), cols(me[1], 0, 4)], l1.at[0, me[1]])]
    own_in += [local(("own", 1 + y), theta_ref.at[pl.ds(hb, hb), cols(y, me[2])],
                     l1.at[1, me[2], pl.ds(0, hb), pl.ds(y * fcol, fcol)]) for y in range(4)]
    own_in.append(local(("own", 5), fact_all.at[pl.ds(0, fact_ref.shape[0]), my], fact_ref))

    with jax.named_scope("in1"):
        first = [in_first(h) for h in range(2)]
        for m in own_in:
            m.start()
        lam_ref[...] = lam_all[pl.ds(0, 1), my]
        mu_ref[...] = mu_all[pl.ds(0, 1), my]
        for relay, finish, started in first:
            relay()
    with jax.named_scope("in2"):
        for m in own_in:
            m.wait()
        second = []
        for h, (relay, finish, started) in enumerate(first):
            finish()
            second.append(in_second(h))
        for v in range(4):
            th[me[2], v, pl.ds(0, hb)] = l1[0, v, pl.ds(0, hb), pl.ds(pl.multiple_of(me[2] * fcol, fcol), fcol)]
            th[v, me[1], pl.ds(hb, hb)] = l1[1, v, pl.ds(0, hb), pl.ds(pl.multiple_of(me[1] * fcol, fcol), fcol)]
        for relay, finish, started in second:
            relay()
        for relay, finish, started in second:
            finish()
        for relay, finish, started in first + second:
            for m in started:
                m.wait_send()
    with jax.named_scope("prep"):
        lax.fori_loop(0, n_panels, first_prep, 0)

    def out_pieces(h, tag):
        if h == 0:
            return halves(tag)
        return (0, 1, 2, 3) if tag[0] == "d" else (2, 3) if tag[1] == "+" else (0, 1)

    def out_first(h):
        d = 2 - h

        def sends(tag):
            way = tag[1] == "+"
            b = 0 if way else 1
            vs = [(v if h == 0 else near[2][v], v % 2) for v in out_pieces(h, tag)]
            if tag[0] == "f":
                return [(rel2.at[h, b, at], m1.at[h, side(d, 3 if way else 1), v]) for v, at in vs]
            to = side(d, {"r": 2, "d": 1 if way else 3}[tag[0]])
            return [(mine(th, h, v, to), m1.at[h, me[d], v] if tag[0] == "d" else rel2.at[h, b, at]) for v, at in vs]
        return relayed(("out1", h), d, sends, begin=False)

    def out_start(o):
        for tag in ((), ("d+",), ("r+", "r-"), ("d-",))[o]:
            for m in out_first(0)[3](tag):
                m.start()
        for tag in ("r+" if o >= 2 else "r-", "d+", "d-"):
            out_first(1)[3](tag)[out_pieces(1, tag).index(o)].start()

    def one_step(step, carry):
        slot = rem(step, 2)
        with jax.named_scope("twait"):
            for r in range(n_panels):
                swap_t(r, slot).wait()
                swap_z(r).wait()

        def products(rows, cols):
            return (lax.dot_general(jnp.concatenate([t_own[slot, r] for r in rows], 0), t_own[slot, cols], NT,
                                    preferred_element_type=F32)
                    + lax.dot_general(jnp.concatenate([t_par[r] for r in rows], 0), t_par[cols], NT,
                                      preferred_element_type=F32))

        def put(m, x, y, z):
            g[0, chip_index(0, x, y, z)] = m[:48]
            g[1, chip_index(1, x, y, z)] = m[48:96]
            g[2, chip_index(2, x, y, z), pl.ds(0, 32)] = m[96:]

        def form(h, cc):
            i = h * 2
            cols = pl.ds(pl.multiple_of(i * B, 2 * B), 2 * B)
            dg = products([cols], cols)
            for t in range(2):
                dt = dg[t * B:(t + 1) * B, t * B:(t + 1) * B]
                d_all[i + t] = dt
                s_all[i + t] = jnp.broadcast_to(jnp.sum(jnp.where(eye, dt, 0.0), axis=0, keepdims=True), (8, B))
            m = products([blk(rem(i + core * kc + 1 + t, nb)) for t in range(kc + 1)], cols)
            y, z = div(h, 2), 2 * rem(h, 2)
            for t in range(kc + 1):
                if t < kc:
                    put(m[t * B:(t + 1) * B, :B], t, y, z)
                if t > 0:
                    put(m[t * B:(t + 1) * B, B:], t - 1, y, z + 1)
            return cc
        with jax.named_scope("form"):
            lax.fori_loop(0, nb // 2, form, 0, unroll=4)

        with jax.named_scope("pair"):
            @pl.when(core == 1)
            def _():
                def pair(t, cc):
                    i = t + nb // 2
                    put(jnp.where(low, d_all[i], d_all[t]), 3, div(i, 4), rem(i, 4))
                    return cc
                lax.fori_loop(0, nb // 2, pair, 0)

        pending = []

        order = (2, 1, 3, 0)
        wave_base = [[[(near[perms[k][0]][t] * 4 + near[perms[k][1]][o]) * 4 for t in range(4)] for o in order]
                     for k in range(3)]

        def wave(k, s):
            return perms[k], 4, order[s], wave_base[k][s]

        def n_waves(k):
            return 4

        def ring_copy(k, s, tag):
            p, n, by, base = wave(k, s)
            ha, hb = split(n, False)
            at, half, kind, to = {
                "m1p": (2, ha, 0, 1), "m1m": (2, hb, 1, 3), "m2p": (1, hb, 2, 1), "m2m": (3, ha, 3, 3),
                "m3p": (1, ha, 2, 1), "m3m": (3, hb, 3, 3)}[tag]
            return copy(("rs", k, s, tag), part_of(g, k, base[at], half), part_of(ring1.at[k], kind, s * n, half),
                        shifted(p[0], to))

        def ring_start(s, tags, colours=(0, 1, 2)):
            for tag in tags:
                for k in colours:
                    if s < n_waves(k):
                        m = ring_copy(k, s, tag)
                        m.start()
                        pending.append(m)

        def ring_merge(s):
            for k in range(3):
                p, n, by, base = wave(k, s)
                ha, hb = split(n, False)
                for got, out, at, half, kind in (("m1p", "m3p", 1, ha, 0), ("m1m", "m3m", 3, hb, 1)):
                    ring_copy(k, s, got).wait_recv()
                    part_of(g, k, base[at], half)[...] += part_of(ring1.at[k], kind, s * n, half)[...]
                    m = ring_copy(k, s, out)
                    m.start()
                    pending.append(m)

        def owner_copy(k, by, s):
            return copy(("rb", k, by), acc2.at[k, pl.ds(s * 4, 4)], dirb.at[k, by], shifted(perms[k][1], by))

        def via_copy(k, b):
            return copy(("rv", k, b), acc2.at[k, pl.ds(2 * b, 2)], relb.at[k, b], shifted(perms[k][1], (1, 3)[b]))

        def ring_finish(s):
            for k in range(3):
                p, n, by, base = wave(k, s)
                for tag in ("m2p", "m2m", "m3p", "m3m"):
                    ring_copy(k, s, tag).wait_recv()
                if by in (1, 3):
                    via_copy(k, by // 2).wait_recv()
                for v in range(n):
                    tot = g[k, base[0] + v] + ring1[k, 2, s * n + v] + ring1[k, 3, s * n + v]
                    if by in (1, 3) and v // 2 == by // 2:
                        tot = tot + relb[k, by // 2, v % 2]
                    acc2[k, s * n + v] = tot
                ms = [via_copy(k, 0), via_copy(k, 1)] if by == 2 else [owner_copy(k, by, s)] if by else []
                for m in ms:
                    m.start()
                    pending.append(m)

        ring_start(0, ("m1p", "m1m"), (0, 1))

        row8 = lax.broadcasted_iota(jnp.int32, (8, B), 0)

        def tails(i, cc):
            y, z = div(i, 4), rem(i, 4)
            for x in range(4):
                off = core * kc + x
                at = chip_index(2, x, y, z)
                g[2, at, pl.ds(32, 8)] = jnp.where(row8 == 0, s_all[rem(i + off + 1, nb)], s_all[i])
                g[2, at, pl.ds(40, 8)] = (zt[pl.ds(pl.multiple_of(off * 8, 8), 8), blk(i)]
                                          + zt_par[pl.ds(x * 8, 8), blk(i)])
            return cc
        with jax.named_scope("tails"):
            lax.fori_loop(0, nb, tails, 0)

        most = 4
        with jax.named_scope("rs0"):
            ring_start(0, ("m1p", "m1m"), (2,))
            ring_start(0, ("m2p", "m2m"))
            ring_start(1, ("m1p", "m1m"))
            for s in range(most):
                ring_merge(s)
                ring_start(s + 1, ("m2p", "m2m"))
                ring_start(s + 2, ("m1p", "m1m"))
                if s:
                    ring_finish(s - 1)
            ring_finish(most - 1)
        last = []
        with jax.named_scope("rs1"):
            for k in range(3):
                p = perms[k]
                n, s = 4, 3
                bys = (1, 3)
                for by in bys:
                    owner_copy(k, by, 0).wait_recv()
                for v in range(n):
                    tot = acc2[k, s * n + v]
                    for by in bys:
                        tot = tot + dirb[k, by, v]
                    acc3[k, v] = tot
                ms = []
                for by in (1, 2, 3):
                    m = copy(("rc", k, by), acc3.at[k, near[p[2]][by]], dir3.at[k, by],
                             shifted(p[2], by))
                    m.start()
                    ms.append(m)
                last.append(ms)
                pending += ms
        with jax.named_scope("rs2"):
            for k in range(3):
                tot = acc3[k, me[perms[k][2]]]
                for m in last[k]:
                    m.wait_recv()
                for by in range(1, len(last[k]) + 1):
                    tot = tot + dir3[k, by]
                unit[k] = tot

        summed = pending
        pending = []
        with jax.named_scope("kunit"):
            packed = unit_of(core, (me[0] * 4 + me[1]) * 4 + me[2])[3]
            g_u = jnp.concatenate([unit[0], unit[1], unit[2, pl.ds(0, 32)]], 0)
            sj = jnp.broadcast_to(unit[2, pl.ds(32, 1)], (B, B))
            si = jnp.broadcast_to(unit[2, pl.ds(33, 1)], (B, B))
            si_c = jnp.broadcast_to(jnp.sum(jnp.where(eye, si, 0.0), axis=1, keepdims=True), (B, B))
            sj_c = jnp.broadcast_to(jnp.sum(jnp.where(eye, sj, 0.0), axis=1, keepdims=True), (B, B))
            lower = jnp.logical_and(packed, low)
            upper = jnp.logical_and(packed, jnp.logical_not(low))
            s_sum = jnp.where(lower, si_c, sj_c) + jnp.where(upper, sj, si)
            dist = jnp.maximum(s_sum - 2.0 * g_u, 0.0)
            k_u = jnp.exp(-dist / kern_width)
            z_u = unit[2, pl.ds(40, 8)]
            pieces = (k_u[:48], k_u[48:96], jnp.concatenate([k_u[96:], z_u, jnp.zeros_like(z_u)], 0))
            own = [chip_index(k, *me) for k in range(3)]
            for k in range(3):
                ag[k, own[k]] = pieces[k].astype(BF16)

        def place(ref, c, k, a, b, at):
            for v in range(4):
                coord = [0, 0, 0]
                for d, t in zip(perms[k], (a, b, v)):
                    coord[d] = t
                off = c * kc + coord[0]
                i = coord[1] * 4 + coord[2]
                top = (rem(i + off + 1, nb) + div(off * nb + i, 2 * n_chip - nb // 2) * (nb // 2)) * B + 48 * k
                n = (48, 48, 32)[k]
                kfull[pl.ds(pl.multiple_of(top, 16), n), blk(i)] = ref[k, at + v, pl.ds(0, n)]
                if k == 2:
                    tail = ref[k, at + v, pl.ds(32, 16)].astype(F32)
                    zt_b[pl.ds(pl.multiple_of(off * 8, 8), 8), blk(i)] = tail[:8]

        chunks = {}

        def chunk(k, ta, tb):
            if (k, ta, tb) not in chunks:
                p = perms[k]
                a, b = near[p[0]][ta], near[p[1]][tb]
                chunks[k, ta, tb] = (a, b, (a * 4 + b) * 4, 4)
            return chunks[k, ta, tb]

        def swap(k, ta, tb):
            a, b, at, n = chunk(k, ta, tb)
            return copy(("sw", k, ta, tb), ag.at[k, pl.ds(at, n)], ag_par.at[k, pl.ds(at, n)], partner)

        swaps = []
        placed = []

        def take(upto):
            while len(placed) < upto:
                k, ta, tb = swaps[len(placed)]
                swap(k, ta, tb).wait_recv()
                a, b, at, n = chunk(k, ta, tb)
                place(ag_par, 1 - core, k, a, b, at)
                placed.append((k, ta, tb))

        def have(k, ta, tb):
            swap(k, ta, tb).start()
            swaps.append((k, ta, tb))
            a, b, at, n = chunk(k, ta, tb)
            place(ag, core, k, a, b, at)

        def unit_copy(stage, k, by, tc, start):
            p = perms[k]
            a, b, at, n = chunk(k, 0, 0)
            at = at + near[p[2]][tc]
            m = copy(("u", stage, k, by, tc), ag.at[k, at], ag.at[k, at], shifted(p[stage], by))
            if start:
                m.start()
                pending.append(m)
            return m

        def a_copy(k, tb, tag, start=False):
            p = perms[k]
            ta, h, to = {"n1p": (0, 0, 1), "n1m": (0, 1, 3), "n2p": (0, 1, 1), "n2m": (0, 0, 3), "n3p": (3, 0, 1),
                         "n3m": (1, 1, 3)}[tag]
            a, b, at, n = chunk(k, ta, tb)
            half = split(n, True)[h]
            m = copy(("a", k, tb, tag), part_of(ag, k, at, half), part_of(ag, k, at, half), shifted(p[0], to))
            if start:
                m.start()
                pending.append(m)
            return m

        def a_launch(k, tb):
            for tag in ("n1p", "n1m", "n2p", "n2m"):
                a_copy(k, tb, tag, True)
            have(k, 0, tb)

        def a_relay(tb):
            for k in range(3):
                if True:
                    for got, out in (("n1p", "n3p"), ("n1m", "n3m")):
                        a_copy(k, tb, got).wait_recv()
                        a_copy(k, tb, out, True)

        def a_near(tb):
            for k in range(3):
                if True:
                    for got, ta in (("n2p", 3), ("n2m", 1)):
                        a_copy(k, tb, got).wait_recv()
                        have(k, ta, tb)

        def a_far(tb):
            for k in range(3):
                if True:
                    for got in ("n3p", "n3m"):
                        a_copy(k, tb, got).wait_recv()
                    have(k, 2, tb)

        def a_waves(tbs):
            for tb in tbs:
                for k in range(3):
                    a_launch(k, tb)

        with jax.named_scope("ag2"):
            for k in range(3):
                for by in (1, 2, 3):
                    unit_copy(2, k, by, 0, True)
            for k in range(3):
                for by in (2, 1, 3):
                    unit_copy(1, k, by, 0, True)
            for m in summed:
                m.wait_send()
            for by in (1, 3, 2):
                for k in range(3):
                    unit_copy(2, k, by, 0, False).wait_recv()
                    for bb in (2, 1, 3):
                        unit_copy(1, k, bb, 4 - by, True)
            a_waves((0,))

        def b_arrivals(bb):
            for k in range(3):
                for tc in range(4):
                    unit_copy(1, k, bb, tc, False).wait_recv()

        with jax.named_scope("ag1"):
            for name, stage, at, got in (("b1", b_arrivals, 1, 0), ("b3", b_arrivals, 3, 0), ("r0", a_relay, 0, 0),
                                         ("w", a_waves, (3, 1), 0), ("b2", b_arrivals, 2, 0), ("w2", a_waves, (2,), 0),
                                         ("n0", a_near, 0, 6), ("r3", a_relay, 3, 9), ("r1", a_relay, 1, 12),
                                         ("n3", a_near, 3, 15), ("r2", a_relay, 2, 18)):
                with jax.named_scope("ag1_" + name):
                    stage(at)
                    take(min(got, len(swaps) - 3))
        with jax.named_scope("ag0"):
            for stage, tb in ((a_far, 0), (a_near, 1), (a_far, 3), (a_near, 2), (a_far, 1), (a_far, 2)):
                before = len(swaps)
                with jax.named_scope("ag0_%s%d" % (stage.__name__, tb)):
                    stage(tb)
                take(before - 12)

        per = 8

        def mirror(c, r, cc):
            at = []
            for t in range(per):
                u, i, j, packed = unit_of(c, r * per + t)
                at.append((i, j, kfull[blk(j), blk(i)].T))
            for i, j, m in at:
                kfull[blk(i), blk(j)] = m
            return cc

        def unpack(r, cc):
            both = []
            for v in range(4):
                i = r * 4 + v + nb // 2
                m = kfull[blk(i), blk(i)].astype(F32)
                mt = m.T
                both.append((jnp.where(eye, 1.0, jnp.where(low, m, mt)), jnp.where(eye, 1.0, jnp.where(low, mt, m))))
            for v, (m, mt) in enumerate(both):
                t = r * 4 + v
                kfull[blk(t + nb // 2), blk(t + nb // 2)] = m.astype(BF16)
                kfull[blk(t), blk(t)] = mt.astype(BF16)
            return cc
        with jax.named_scope("mirror1"):
            lax.fori_loop(0, div(n_chip - core * (nb // 2), per), functools.partial(mirror, core), 0)
        with jax.named_scope("swapwait"):
            take(len(swaps))
        with jax.named_scope("mirror2"):
            lax.fori_loop(0, div(n_chip - (1 - core) * (nb // 2), per), functools.partial(mirror, 1 - core), 0)
            lax.fori_loop(0, nb // 8, unpack, 0)

        def grads(r, cc):
            lowt = lax.dot_general(zt_b[:, panel(r)].astype(BF16), fact_ref[...], TN, preferred_element_type=F32)
            a_buf[panel(r)] = (-((get_rows(r) - mu_ref[...]) * lam_ref[...] + lowt)).astype(BF16)
            return cc
        with jax.named_scope("grads"):
            lax.fori_loop(0, n_panels, grads, 0, unroll=2)

        def update(h, cc):
            done = []
            for t in range(2):
                r = rem(me[2] + 2 + 2 * h + t, 4)
                kr = kfull[panel(r)]
                mass = jnp.sum(kr.astype(F32), axis=1, keepdims=True)
                drive = jnp.dot(kr, a_buf[...], preferred_element_type=F32)
                pull = jnp.dot(kr, t_own[slot], preferred_element_type=F32)
                upd = (drive + (2.0 / kern_width) * (mass * t_own[slot, panel(r)].astype(F32) - pull)) / n_total
                theta = get_rows(r) + step_size * upd
                for v in range(4):
                    th[r, v] = theta[v * B:(v + 1) * B]
                done.append(r)

            @pl.when(step < NUM_STEPS - 1)
            def _():
                for r in done:
                    prepare(r, get_rows(r), 1 - slot)

            for o in range(4):
                @pl.when(jnp.logical_and(step == NUM_STEPS - 1, h == (o + 2) % 4 // 2))
                def _():
                    out_start(o)
            return cc
        with jax.named_scope("update"):
            lax.fori_loop(0, n_panels // 2, update, 0)
        with jax.named_scope("sendwait"):
            for m in pending:
                m.wait_send()
            for k, ta, tb in swaps:
                swap(k, ta, tb).wait_send()
        return carry

    lax.fori_loop(0, NUM_STEPS, one_step, 0)

    def out_second(h):
        d = 1 + h

        def place_of(src_at, v):
            return out_ref.at[pl.ds(h * hb, hb), cols(src_at, v) if h == 0 else cols(v, src_at)]

        def sends(tag):
            way = tag[1] == "+"
            b = 0 if way else 1
            if tag[0] == "f":
                return [(rel3.at[h, b, t], place_of(side(d, 3 if way else 1), 2 * b + t)) for t in range(2)]
            to = side(d, {"r": 2, "d": 1 if way else 3}[tag[0]])
            if tag[0] == "r":
                return [(m1.at[h, v, to], rel3.at[h, b, v % 2]) for v in halves(tag)]
            return [(m1.at[h, v, to], place_of(me[d], v)) for v in range(4)]
        return relayed(("out2", h), d, sends)

    with jax.named_scope("out1"):
        first = [out_first(h)[:3] for h in range(2)]
        for v in range(4):
            m1[0, me[2], v] = th[me[2], v, pl.ds(0, hb)]
            m1[1, me[1], v] = th[v, me[1], pl.ds(hb, hb)]
        for relay, finish, started in first:
            relay()
    with jax.named_scope("out2"):
        second = []
        for h, (relay, finish, started) in enumerate(first):
            finish()
            second.append(out_second(h))
        own_out = []
        for v in range(4):
            own_out.append(local(("back", v), m1.at[0, v, me[1]], out_ref.at[pl.ds(0, hb), cols(me[1], v)]))
            own_out.append(local(("back", 4 + v), m1.at[1, v, me[2]], out_ref.at[pl.ds(hb, hb), cols(v, me[2])]))
        for m in own_out:
            m.start()
        for relay, finish, started in second:
            relay()
        for relay, finish, started in second:
            finish()
        for relay, finish, started in first + second:
            for m in started:
                m.wait_send()
        for m in own_out:
            m.wait()


def run_steps(theta, lam, mu, fac, sizes, kern_width, step_size):
    n_total, fcol = theta.shape[0] * sizes[1] * sizes[2], theta.shape[1] // (sizes[1] * sizes[2])
    rank = fac.shape[1]
    nb = n_total // B
    n_chip = sizes[0] * sizes[1] * sizes[2]
    assert nb * nb == 4 * n_chip and rank == 4 * nb
    hb = B // 2
    cfg = dict(sizes=sizes, nb=nb, kern_width=kern_width, step_size=step_size)
    n1, n2 = n_chip, n_chip
    vmem = pl.BlockSpec(memory_space=pltpu.VMEM)
    most1 = max(n_chip // sizes[k] for k in range(3))
    most2 = max(sizes)
    blocks = (4, 4, B, fcol)
    scratch = [
        pltpu.VMEM(blocks, F32),
        pltpu.VMEM((2, 4, hb, 4 * fcol), F32),
        pltpu.VMEM((2, 4, 4, hb, fcol), F32),
        pltpu.VMEM((2, 2, hb // 2, 4 * fcol), F32),
        pltpu.VMEM((2, 2, 2, hb, fcol), F32),
        pltpu.VMEM((2, 2, 2, hb, fcol), F32),
        pltpu.VMEM((1, fcol), F32),
        pltpu.VMEM((1, fcol), F32),
        pltpu.VMEM((rank, fcol), BF16),
        pltpu.VMEM((2, n_total, fcol), BF16),
        pltpu.VMEM((n_total, fcol), BF16),
        pltpu.VMEM((n_total, fcol), BF16),
        pltpu.VMEM((rank, n_total), F32),
        pltpu.VMEM((rank // 2, n_total), F32),
        pltpu.VMEM((rank, n_total), F32),
        pltpu.VMEM((nb, 8, B), F32),
        pltpu.VMEM((nb, B, B), F32),
        pltpu.VMEM((3, n_chip, PIECE, B), F32),
        pltpu.VMEM((3, 4, most1, PIECE, B), F32),
        pltpu.VMEM((3, 2, 2, PIECE, B), F32),
        pltpu.VMEM((3, 4, most2, PIECE, B), F32),
        pltpu.VMEM((3, 4, PIECE, B), F32),
        pltpu.VMEM((3, most1, PIECE, B), F32),
        pltpu.VMEM((3, most2, PIECE, B), F32),
        pltpu.VMEM((3, PIECE, B), F32),
        pltpu.VMEM((3, n_chip, PIECE, B), BF16),
        pltpu.VMEM((3, n_chip, PIECE, B), BF16),
        pltpu.VMEM((n_total, n_total), BF16),
        pltpu.SemaphoreType.DMA((NUM_SEMS,)),
        pltpu.SemaphoreType.DMA((NUM_SEMS,)),
    ]
    hbm = pl.BlockSpec(memory_space=pltpu.HBM)
    return pl.pallas_call(
        functools.partial(steps_kernel, cfg),
        out_shape=jax.ShapeDtypeStruct(theta.shape, F32),
        in_specs=[hbm, vmem, vmem, hbm],
        out_specs=hbm,
        scratch_shapes=scratch,
        compiler_params=pltpu.CompilerParams(collective_id=0, has_side_effects=True, vmem_limit_bytes=60 * 1024 * 1024),
        name="svgd_steps",
    )(theta, lam[None], mu[None], fac.T)


def solution(mesh, sizes=(4, 4, 4)):
    part_size = mesh.shape["part"]
    feat_size = mesh.shape["feat"]

    def local_steps(local_theta, prec_loc, mean_loc, factor_loc):
        rows_loc, feat_loc = local_theta.shape
        n_total = rows_loc * part_size
        feat_total = feat_loc * feat_size
        kern_width = 2.0 * feat_total / math.log(n_total)
        step_size = 0.15 * n_total * feat_total / math.log(n_total)
        return run_steps(local_theta, prec_loc, mean_loc, factor_loc, sizes, kern_width, step_size)

    row_spec = P(("ens", "part"), "feat")
    vec_spec = P(("ens", "feat"))
    fac_spec = P(("ens", "feat"), None)
    return jax.shard_map(local_steps, mesh=mesh, in_specs=(row_spec, vec_spec, vec_spec, fac_spec), out_specs=row_spec, check_vma=False)
```

profile of v0, /device:TPU:0, one launch (start us, length us, event | category | flops | bytes accessed | tf_op | source)
XLA Modules:
  0.0 233.8 jit_solution(218205441193820064)
XLA Ops:
  0.0 230.7 %svgd_steps.1 = f32[128,4096]{1,0:T(8,128)} custom-call(f32[128,4096]{1,0:T(8,128)} %theta_ref.1, f32[1,4096]{1,0:T(1,128)} %bitcast.4, f32[1,4096]{1,0:T(1,128)} %bitcast.5, bf16[64,4096]{1,0:T(8,128)(2,1)} %bitcast.3), custom_call_target="tpu_custom_call" | custom-call | tf_op jit(solution)/shard_map/svgd_steps/pallas_call | solution.py:770
  230.7 3.1 %copy.6 = f32[128,4096]{1,0:T(8,128)} copy(f32[128,4096]{1,0:T(8,128)} %svgd_steps.1) | data formatting | bytes 4194304
where the time goes:
time: 234 us
  Pallas kernels  231 us (99%)
  local copies, waits for them, and re-layouts  3.11 us (1%)
    pallas_call x1, Pallas kernels, run_steps(): pl.pallas_call(functools.partial(steps_kernel, cfg), out_shape=jax.ShapeD...  231 us

commit v1 on v0

--- a/solution.py
+++ b/solution.py
@@ -181,7 +181,7 @@
         else:
             for tag in ("r+", "r-", "d+", "d-"):
                 started += copies(tag)
-        return (relay, finish, started) if begin else (relay, finish, started, copies)
+        return relay, finish, started, copies
 
     def halves(tag):
         if tag[0] == "d":
@@ -210,19 +210,56 @@
             return [(theta_ref.at[rows, cols(y, to)], dst(y, 1)) for y in range(4)]
         return relayed(("in1", h), d, sends)
 
+    def pieces(tag):
+        return (0, 3, 1, 2) if tag[0] == "d" else (0, 3) if tag[1] == "+" else (1, 2)
+
+    def start_piece(leg, o):
+        for tag in ("r+" if o in (0, 3) else "r-", "d+", "d-"):
+            leg[3](tag)[pieces(tag).index(o)].start()
+
+    def two_legs(first, second):
+        for h in range(2):
+            first[h][0]()
+        for tag, o in (("d+", 3), ("d-", 1)):
+            for h in range(2):
+                for m in first[h][3](tag):
+                    m.wait_recv()
+                start_piece(second[h], o)
+        for h in range(2):
+            for tag in ("f+", "f-"):
+                for m in first[h][3](tag):
+                    m.wait_recv()
+            start_piece(second[h], 2)
+
+    def close(first, second):
+        for h in range(2):
+            second[h][0]()
+        for h in range(2):
+            second[h][1]()
+        for leg in first + second:
+            for m in leg[2]:
+                m.wait_send()
+
     def in_second(h):
         d = 2 - h
 
         def sends(tag):
             way = tag[1] == "+"
             b = 0 if way else 1
-            if tag[0] == "f":
-                return [(rel2.at[h, b, v % 2], mine(th, h, v, side(d, 3 if way else 1))) for v in halves(tag)]
-            to = side(d, {"r": 2, "d": 1 if way else 3}[tag[0]])
-            at = pl.ds(pl.multiple_of(to * fcol, fcol), fcol)
-            return [(l1.at[h, v, pl.ds(0, hb), at], mine(th, h, v, me[d]) if tag[0] == "d" else rel2.at[h, b, v % 2])
-                    for v in halves(tag)]
-        return relayed(("in2", h), d, sends)
+            out = []
+            to = side(d, {"r": 2, "d": 1 if way else 3, "f": 0}[tag[0]])
+            for at, o in enumerate(pieces(tag)):
+                v = near[1 + h][o]
+                if tag[0] == "f":
+                    out.append((rel2.at[h, b, at], mine(th, h, v, side(d, 3 if way else 1))))
+                    continue
+                if o == 0:
+                    src = theta_ref.at[pl.ds(h * hb, hb), cols(me[1], to) if h == 0 else cols(to, me[2])]
+                else:
+                    src = l1.at[h, v, pl.ds(0, hb), pl.ds(pl.multiple_of(to * fcol, fcol), fcol)]
+                out.append((src, mine(th, h, v, me[d]) if tag[0] == "d" else rel2.at[h, b, at]))
+            return out
+        return relayed(("in2", h), d, sends, begin=False)
 
     own_in = [local(("own", 0), theta_ref.at[pl.ds(0, hb), cols(me[1], 0, 4)], l1.at[0, me[1]])]
     own_in += [local(("own", 1 + y), theta_ref.at[pl.ds(hb, hb), cols(y, me[2])],
@@ -231,29 +268,22 @@
 
     with jax.named_scope("in1"):
         first = [in_first(h) for h in range(2)]
+        second = [in_second(h) for h in range(2)]
         for m in own_in:
             m.start()
+        for h in range(2):
+            start_piece(second[h], 0)
         lam_ref[...] = lam_all[pl.ds(0, 1), my]
         mu_ref[...] = mu_all[pl.ds(0, 1), my]
-        for relay, finish, started in first:
-            relay()
     with jax.named_scope("in2"):
+        two_legs(first, second)
         for m in own_in:
             m.wait()
-        second = []
-        for h, (relay, finish, started) in enumerate(first):
-            finish()
-            second.append(in_second(h))
         for v in range(4):
             th[me[2], v, pl.ds(0, hb)] = l1[0, v, pl.ds(0, hb), pl.ds(pl.multiple_of(me[2] * fcol, fcol), fcol)]
             th[v, me[1], pl.ds(hb, hb)] = l1[1, v, pl.ds(0, hb), pl.ds(pl.multiple_of(me[1] * fcol, fcol), fcol)]
-        for relay, finish, started in second:
-            relay()
-        for relay, finish, started in second:
-            finish()
-        for relay, finish, started in first + second:
-            for m in started:
-                m.wait_send()
+        close(first, second)
+
     with jax.named_scope("prep"):
         lax.fori_loop(0, n_panels, first_prep, 0)
 
@@ -684,39 +714,35 @@
         def sends(tag):
             way = tag[1] == "+"
             b = 0 if way else 1
-            if tag[0] == "f":
-                return [(rel3.at[h, b, t], place_of(side(d, 3 if way else 1), 2 * b + t)) for t in range(2)]
-            to = side(d, {"r": 2, "d": 1 if way else 3}[tag[0]])
-            if tag[0] == "r":
-                return [(m1.at[h, v, to], rel3.at[h, b, v % 2]) for v in halves(tag)]
-            return [(m1.at[h, v, to], place_of(me[d], v)) for v in range(4)]
-        return relayed(("out2", h), d, sends)
+            out = []
+            to = side(d, {"r": 2, "d": 1 if way else 3, "f": 0}[tag[0]])
+            for at, o in enumerate(pieces(tag)):
+                v = near[2 - h][o]
+                if tag[0] == "f":
+                    out.append((rel3.at[h, b, at], place_of(side(d, 3 if way else 1), v)))
+                    continue
+                src = mine(th, h, to, me[2 - h]) if o == 0 else m1.at[h, v, to]
+                out.append((src, place_of(me[d], v) if tag[0] == "d" else rel3.at[h, b, at]))
+            return out
+        return relayed(("out2", h), d, sends, begin=False)
 
     with jax.named_scope("out1"):
-        first = [out_first(h)[:3] for h in range(2)]
+        first = [out_first(h) for h in range(2)]
+        second = [out_second(h) for h in range(2)]
+        for h in range(2):
+            start_piece(second[h], 0)
         for v in range(4):
             m1[0, me[2], v] = th[me[2], v, pl.ds(0, hb)]
             m1[1, me[1], v] = th[v, me[1], pl.ds(hb, hb)]
-        for relay, finish, started in first:
-            relay()
     with jax.named_scope("out2"):
-        second = []
-        for h, (relay, finish, started) in enumerate(first):
-            finish()
-            second.append(out_second(h))
+        two_legs(first, second)
         own_out = []
         for v in range(4):
             own_out.append(local(("back", v), m1.at[0, v, me[1]], out_ref.at[pl.ds(0, hb), cols(me[1], v)]))
             own_out.append(local(("back", 4 + v), m1.at[1, v, me[2]], out_ref.at[pl.ds(hb, hb), cols(v, me[2])]))
         for m in own_out:
             m.start()
-        for relay, finish, started in second:
-            relay()
-        for relay, finish, started in second:
-            finish()
-        for relay, finish, started in first + second:
-            for m in started:
-                m.wait_send()
+        close(first, second)
         for m in own_out:
             m.wait()
 

time: 234 us -> 233 us (level)
  no operation moved by 1% of the time
where the time goes in v1:
time: 233 us; the launch traced here: 232 us
  Pallas kernels  229 us (98%)
  local copies, waits for them, and re-layouts  3.11 us (1%)
    pallas_call x1, Pallas kernels, run_steps(): pl.pallas_call(functools.partial(steps_kernel, cfg), out_shape=jax.ShapeD...  229 us

profile of v1, /device:TPU:0, one launch (start us, length us, event | category | flops | bytes accessed | tf_op | source)
XLA Modules:
  0.0 232.3 jit_solution(4720864288769556853)
XLA Ops:
  0.0 229.2 %svgd_steps.1 = f32[128,4096]{1,0:T(8,128)} custom-call(f32[128,4096]{1,0:T(8,128)} %theta_ref.1, f32[1,4096]{1,0:T(1,128)} %bitcast.4, f32[1,4096]{1,0:T(1,128)} %bitcast.5, bf16[64,4096]{1,0:T(8,128)(2,1)} %bitcast.3), custom_call_target="tpu_custom_call" | custom-call | tf_op jit(solution)/shard_map/svgd_steps/pallas_call | solution.py:796
  229.2 3.1 %copy.6 = f32[128,4096]{1,0:T(8,128)} copy(f32[128,4096]{1,0:T(8,128)} %svgd_steps.1) | data formatting | bytes 4194304

commit v2 on v1

--- a/solution.py
+++ b/solution.py
@@ -619,9 +619,9 @@
 
         with jax.named_scope("ag1"):
             for name, stage, at, got in (("b1", b_arrivals, 1, 0), ("b3", b_arrivals, 3, 0), ("r0", a_relay, 0, 0),
-                                         ("w", a_waves, (3, 1), 0), ("b2", b_arrivals, 2, 0), ("w2", a_waves, (2,), 0),
-                                         ("n0", a_near, 0, 6), ("r3", a_relay, 3, 9), ("r1", a_relay, 1, 12),
-                                         ("n3", a_near, 3, 15), ("r2", a_relay, 2, 18)):
+                                         ("w", a_waves, (3, 1), 0), ("b2", b_arrivals, 2, 0), ("w2", a_waves, (2,), 3),
+                                         ("r3", a_relay, 3, 3), ("n0", a_near, 0, 6), ("r1", a_relay, 1, 9),
+                                         ("r2", a_relay, 2, 12), ("n3", a_near, 3, 15)):
                 with jax.named_scope("ag1_" + name):
                     stage(at)
                     take(min(got, len(swaps) - 3))

time: 233 us -> 232 us (level)
  no operation moved by 1% of the time
where the time goes in v2:
time: 232 us; the launch traced here: 231 us
  Pallas kernels  228 us (98%)
  local copies, waits for them, and re-layouts  3.11 us (1%)
    pallas_call x1, Pallas kernels, run_steps(): pl.pallas_call(functools.partial(steps_kernel, cfg), out_shape=jax.ShapeD...  228 us

profile of v2, /device:TPU:0, one launch (start us, length us, event | category | flops | bytes accessed | tf_op | source)
XLA Modules:
  0.0 231.4 jit_solution(1499973263604676394)
XLA Ops:
  0.0 228.3 %svgd_steps.1 = f32[128,4096]{1,0:T(8,128)} custom-call(f32[128,4096]{1,0:T(8,128)} %theta_ref.1, f32[1,4096]{1,0:T(1,128)} %bitcast.4, f32[1,4096]{1,0:T(1,128)} %bitcast.5, bf16[64,4096]{1,0:T(8,128)(2,1)} %bitcast.3), custom_call_target="tpu_custom_call" | custom-call | tf_op jit(solution)/shard_map/svgd_steps/pallas_call | solution.py:796
  228.3 3.1 %copy.6 = f32[128,4096]{1,0:T(8,128)} copy(f32[128,4096]{1,0:T(8,128)} %svgd_steps.1) | data formatting | bytes 4194304
